TPU v7x, 256 devices: a whole 4x4x8 slice. The times are simulated.
256 devices in a mesh: seq: 32 (over x, z_hi, y), tp: 8 (over z_lo, core).
Axes of the slice: x: 4, y: 4, z: 8 (z_hi: 2, z_lo: 4; z = z_hi * 4 + z_lo), core: 2. Of those that a mesh axis runs over, the one named last changes fastest.
Arguments:
- latent: bfloat16 [2, 32, 1024, 1152], P(None, 'seq', 'tp'), may hold values from -6 to 6
- modulation: float32 [2, 9, 1152], replicated, may hold values from -4 to 4
- qkv_spatial: bfloat16 [3, 1152, 1152], P(None, None, 'tp'), may hold values from -0.1875 to 0.1875
- gain_spatial: float32 [2, 72], replicated, may hold values from 0.5 to 1.7
- out_spatial: bfloat16 [1152, 1152], P('tp'), may hold values from -0.1875 to 0.1875
- qkv_temporal: bfloat16 [3, 1152, 1152], P(None, None, 'tp'), may hold values from -0.1875 to 0.1875
- gain_temporal: float32 [2, 72], replicated, may hold values from 0.5 to 1.7
- out_temporal: bfloat16 [1152, 1152], P('tp'), may hold values from -0.1875 to 0.1875
- fc_in: bfloat16 [1152, 4608], P(None, 'tp'), may hold values from -0.1875 to 0.1875
- fc_out: bfloat16 [4608, 1152], P('tp'), may hold values from -0.09375 to 0.09375
Outputs:
- result: bfloat16 [2, 32, 1024, 1152], P(None, 'seq', 'tp')
All inputs are finite; a program needn't handle non-finite values.
Results may differ from a plain program's by a relative error of at most 0.017.
Values may be sent and summed in bfloat16 or wider, within the bound.
A program may use at most 64 MiB of HBM per device.

v0:
```python
import math
import jax
import jax.numpy as jnp
from jax import lax
from jax.sharding import PartitionSpec as P

D = 1152
H = 16
epsilon = 1e-06


def layer_norm(values):
    average = jnp.mean(values, axis=-1, keepdims=True)
    centred = values - average
    variance = jnp.mean(centred * centred, axis=-1, keepdims=True)
    return centred * lax.rsqrt(variance + epsilon)


def modulated(field, modulation, offset):
    shift_row = modulation[:, offset][:, None, None, :]
    scale_row = modulation[:, offset + 1][:, None, None, :]
    return (layer_norm(field) * (1.0 + scale_row) + shift_row).astype(jnp.bfloat16)


def project_heads(rows_piece, table, gains, head_dim):
    results = []
    for which_part in range(3):
        projected = jnp.einsum(
            "bfpd,de->bfpe", rows_piece, table[which_part], preferred_element_type=jnp.float32
        )
        if which_part < 2:
            shaped = projected.reshape(
                projected.shape[:-1] + (projected.shape[-1] // head_dim, head_dim)
            )
            shaped = (
                shaped
                * lax.rsqrt(jnp.mean(shaped * shaped, axis=-1, keepdims=True) + epsilon)
                * gains[which_part]
            )
            projected = shaped.reshape(projected.shape)
        results.append(projected.astype(jnp.bfloat16))
    return jnp.stack(results)


def attend(query_rows, key_rows, value_rows, head_dim):
    groups, length, feature_width = query_rows.shape
    head_count = feature_width // head_dim
    query_heads = query_rows.reshape(groups, length, head_count, head_dim)
    key_heads = key_rows.reshape(groups, length, head_count, head_dim)
    value_heads = value_rows.reshape(groups, length, head_count, head_dim)
    block_rows = min(length, 512)

    def one_block(first_row):
        query_block = lax.dynamic_slice_in_dim(query_heads, first_row, block_rows, 1)
        scores = jnp.einsum(
            "gqhe,gkhe->ghqk", query_block, key_heads, preferred_element_type=jnp.float32
        ) / math.sqrt(head_dim)
        weights = jnp.exp(scores)
        probabilities = (weights / jnp.sum(weights, axis=-1, keepdims=True)).astype(jnp.bfloat16)
        return jnp.einsum(
            "ghqk,gkhe->gqhe", probabilities, value_heads, preferred_element_type=jnp.float32
        ).astype(jnp.bfloat16)

    starts = jnp.arange(length // block_rows, dtype=jnp.int32) * block_rows
    pieces = lax.map(one_block, starts)
    return pieces.transpose(1, 0, 2, 3, 4).reshape(groups, length, feature_width)


def frame_attention(query_rows, key_rows, value_rows, head_dim):
    batches, frames, patches, feature_width = query_rows.shape
    members = [
        item.transpose(0, 2, 1, 3).reshape(batches * patches, frames, feature_width)
        for item in (query_rows, key_rows, value_rows)
    ]
    mixed_heads = attend(members[0], members[1], members[2], head_dim)
    return mixed_heads.reshape(batches, patches, frames, feature_width).transpose(0, 2, 1, 3)


def body(
    latent,
    modulation,
    qkv_spatial,
    gain_spatial,
    out_spatial,
    qkv_temporal,
    gain_temporal,
    out_temporal,
    fc_in,
    fc_out,
):
    head_dim = D // H
    running = latent.astype(jnp.float32)
    normed = modulated(running, modulation, 0)
    packed = project_heads(
        lax.all_gather(normed, "tp", axis=2, tiled=True), qkv_spatial, gain_spatial, head_dim
    )
    batches, frames, patches, local_width = packed.shape[1:]
    mixed_heads = attend(
        packed[0].reshape(batches * frames, patches, local_width),
        packed[1].reshape(batches * frames, patches, local_width),
        packed[2].reshape(batches * frames, patches, local_width),
        head_dim,
    )
    mixed_heads = mixed_heads.reshape(batches, frames, patches, local_width)
    partial_value = jnp.einsum(
        "bfpe,ed->bfpd", mixed_heads, out_spatial, preferred_element_type=jnp.float32
    )
    spatial_out = lax.psum_scatter(
        partial_value.astype(jnp.bfloat16), "tp", scatter_dimension=2, tiled=True
    )
    running = running + modulation[:, 2][:, None, None, :] * spatial_out.astype(jnp.float32)
    normed = modulated(running, modulation, 3)
    moved_rows = lax.all_to_all(normed, "seq", split_axis=2, concat_axis=1, tiled=True)
    packed = project_heads(
        lax.all_gather(moved_rows, "tp", axis=2, tiled=True), qkv_temporal, gain_temporal, head_dim
    )
    mixed_heads = frame_attention(packed[0], packed[1], packed[2], head_dim)
    partial_value = jnp.einsum(
        "bfpe,ed->bfpd", mixed_heads, out_temporal, preferred_element_type=jnp.float32
    )
    shares = lax.psum_scatter(
        partial_value.astype(jnp.bfloat16), "tp", scatter_dimension=2, tiled=True
    )
    temporal_out = lax.all_to_all(shares, "seq", split_axis=1, concat_axis=2, tiled=True)
    running = running + modulation[:, 5][:, None, None, :] * temporal_out.astype(jnp.float32)
    normed = modulated(running, modulation, 6)
    projected = jnp.einsum(
        "bfpd,de->bfpe",
        lax.all_gather(normed, "tp", axis=2, tiled=True),
        fc_in,
        preferred_element_type=jnp.float32,
    )
    hidden = jax.nn.gelu(projected, approximate=True).astype(jnp.bfloat16)
    partial_value = jnp.einsum("bfpe,ed->bfpd", hidden, fc_out, preferred_element_type=jnp.float32)
    mlp_out = lax.psum_scatter(
        partial_value.astype(jnp.bfloat16), "tp", scatter_dimension=2, tiled=True
    )
    return (running + modulation[:, 8][:, None, None, :] * mlp_out.astype(jnp.float32)).astype(
        jnp.bfloat16
    )


def solution(mesh):
    placed = (
        P(None, "seq", "tp", None),
        P(),
        P(None, None, "tp"),
        P(),
        P("tp", None),
        P(None, None, "tp"),
        P(),
        P("tp", None),
        P(None, "tp"),
        P("tp", None),
    )
    return jax.shard_map(
        body, mesh=mesh, in_specs=placed, out_specs=P(None, "seq", "tp", None), check_vma=False
    )
```

profile of v0, /device:TPU:4, one launch (start us, length us, event | category | flops | bytes accessed | tf_op | source)
XLA Modules:
  0.0 529.5 jit_solution(16318409083778460695)
XLA Ops:
  6.5 0.9 slice_bitcast_fusion.1
  7.5 1.2 convert_reduce_fusion
  8.7 1.4 fusion.58
  10.1 2.2 fusion.61
  12.6 62.3 %all-gather.4.cloned.1.call-done = bf16[2,1,1024,1152]{3,2,0,1:T(8,128)(2,1)} async-done(((bf16[2,1,128,1152]{3,2,0,1:T(8,128)(2,1)}), bf16[2,1,1024,1152]{3,2,0,1:T(8,128)(2,1)}) %all-gather.4.cloned.1.call-update) | async-done | bytes 4718608 | tf_op jit(solution)/shard_map/all_gather | solution.py:95
  74.8 5.1 fusion.93
  79.9 1.4 reduce_sum.111
  81.3 5.5 %fusion.94 = (f32[2,1024,144]{1,2,0:T(8,128)}, f32[2,1024,144]{1,2,0:T(8,128)}) fusion(bf16[3,1152,144]{1,2,0:T(8,128)(2,1)} %param.14, bf16[2,1,1024,1152]{3,2,0,1:T(8,128)(2,1)} %all-gather.4.cloned.1.call-done), kind=kOutput, calls=%fused_computation.130 | convolution fusion | flops 679772160 | bytes 7409664 | tf_op jit(solution)/shard_map/bfpd,de->bfpe/dot_general | solution.py:28
  86.8 1.4 reduce_sum.112
  88.4 1.0 copy-done.4
  89.7 4.9 fusion.55
  94.6 12.8 %while.2 = (s32[]{:T(128)}, bf16[2,2,512,2,72]{2,4,3,1,0:T(8,128)(2,1)S(1)}, s32[2]{0:T(128)S(1)}, bf16[2,1024,2,72]{1,3,2,0:T(8,128)(2,1)S(1)}, bf16[2,1024,2,7...) while((s32[]{:T(128)}, ...), condition=%wide.region_6.7_spmd, body=%wide.region_4.6_spmd.sunk | while | flops 614610944 | bytes 20922552 | solution.py:65
  97.2 1.9 fusion.108
  99.1 1.9 fusion.109
  103.6 1.9 fusion.108
  105.5 1.9 fusion.109
  108.5 3.7 fusion.27
  112.3 58.9 %reduce-scatter.4.cloned.1.call-done = bf16[2,1,128,1152]{3,2,0,1:T(8,128)(2,1)} async-done(((bf16[2,1,1024,1152]{3,2,0,1:T(8,128)(2,1)}), bf16[2,1,128,1152]{3,2,0,1:T(8,128)(2,1)}) %reduce-scatter.4.cloned.1.call-update) | async-done | bytes 589840 | tf_op jit(solution)/shard_map/reduce_scatter | solution.py:108
  171.2 1.4 fusion.73
  172.6 1.4 multiply_reduce_fusion.3
  175.1 27.1 %all_to_all.21 = bf16[2,1,128,1152]{3,0,1,2:T(2,128)(2,1)S(1)} all-to-all(bf16[2,1,128,1152]{3,0,1,2:T(2,128)(2,1)S(1)} %copy.73), channel_id=1, replica_groups=mesh['seq'=32,'tp'=8] {'seq'}, dimensions={2} | all-to-all | bytes 1179648 | tf_op jit(solution)/shard_map/all_to_all | solution.py:113
  204.2 56.9 %all-gather.6.cloned.1.call-done = bf16[2,32,32,1152]{3,1,0,2:T(8,128)(2,1)} async-done(((bf16[2,32,4,1152]{3,1,0,2:T(8,128)(2,1)}), bf16[2,32,32,1152]{3,1,0,2:T(8,128)(2,1)}) %all-gather.6.cloned.1.call-update) | async-done | bytes 4718608 | tf_op jit(solution)/shard_map/all_gather | solution.py:115
  261.0 3.9 fusion.49
  265.0 1.4 reshape_reshape.10
  266.4 3.7 multiply_reduce_fusion
  270.1 3.7 multiply_reduce_fusion.1
  273.8 2.4 multiply_convert_fusion
  276.3 1.2 copy.80
  277.4 1.5 convert_element_type.119
  278.9 1.8 copy.81
  280.7 1.4 reshape_reshape.12
  282.1 2.4 copy.77
  284.5 1.5 convert_element_type.117
  286.0 1.8 copy.78
  287.8 1.4 reshape_reshape.11
  289.3 2.4 fusion.38
  292.4 1.1 copy.86
  293.5 1.5 reshape_reshape_transpose.3
  295.0 3.3 convolution_convert_fusion.1
  298.2 3.8 copy.88
  302.1 58.9 %reduce-scatter.6.cloned.1.call-done = bf16[2,32,4,1152]{3,1,0,2:T(8,128)(2,1)} async-done(((bf16[2,32,32,1152]{3,1,0,2:T(8,128)(2,1)}), bf16[2,32,4,1152]{3,1,0,2:T(8,128)(2,1)}) %reduce-scatter.6.cloned.1.call-update) | async-done | bytes 589840 | tf_op jit(solution)/shard_map/reduce_scatter | solution.py:121
  360.9 1.5 copy.89
  362.4 27.1 %all_to_all.22 = bf16[2,32,4,1152]{3,2,0,1:T(4,128)(2,1)S(1)} all-to-all(bf16[2,32,4,1152]{3,2,0,1:T(4,128)(2,1)S(1)} %copy.89), channel_id=1, replica_groups=mesh['seq'=32,'tp'=8] {'seq'}, dimensions={1} | all-to-all | bytes 1179648 | tf_op jit(solution)/shard_map/all_to_all | solution.py:124
  391.3 1.1 add_convert_fusion.1
  392.5 57.9 %all-gather.8.cloned.1.call-done = bf16[2,1,1024,1152]{3,2,0,1:T(8,128)(2,1)} async-done(((bf16[2,1,128,1152]{3,2,0,1:T(8,128)(2,1)}), bf16[2,1,1024,1152]{3,2,0,1:T(8,128)(2,1)}) %all-gather.8.cloned.1.call-update) | async-done | bytes 4718608 | tf_op jit(solution)/shard_map/all_gather | solution.py:129
  450.4 11.3 %fusion.28 = bf16[2,1,1024,1152]{3,2,0,1:T(8,128)(2,1)} fusion(bf16[2,1,1024,1152]{3,2,0,1:T(8,128)(2,1)} %all-gather.8.cloned.1.call-done, bf16[576,1152]{1,0:T(8,128)(2,1)S(1)} %copy-done, bf16[1152,576]{0,1:T(8,128)(2,1)} %param.20), kind=kOutput, calls=%fused_computation.34 | convolution fusion | flops 5448794112 | bytes 12091392 | tf_op jit(solution)/shard_map/bfpe,ed->bfpd/dot_general | solution.py:134
  461.7 58.9 %reduce-scatter.8.cloned.1.call-done = bf16[2,1,128,1152]{3,2,0,1:T(8,128)(2,1)} async-done(((bf16[2,1,1024,1152]{3,2,0,1:T(8,128)(2,1)}), bf16[2,1,128,1152]{3,2,0,1:T(8,128)(2,1)}) %reduce-scatter.8.cloned.1.call-update) | async-done | bytes 589840 | tf_op jit(solution)/shard_map/reduce_scatter | solution.py:135
  520.6 2.0 fusion.74
  (72 shorter events, 8.6 us)
Async XLA Ops:
  6.5 443.8 %copy-start = (bf16[576,1152]{1,0:T(8,128)(2,1)S(1)}, bf16[576,1152]{1,0:T(8,128)(2,1)}, u32[]{:S(2)}) copy-start(bf16[576,1152]{1,0:T(8,128)(2,1)} %param.21) | copy-start | bytes 3981316
  6.5 5.8 %copy-start.10 = (f32[2,72]{1,0:T(2,128)S(1)}, f32[2,72]{1,0:T(2,128)}, u32[]{:S(2)}) copy-start(f32[2,72]{1,0:T(2,128)} %param.15) | copy-start | bytes 1732
  6.5 68.3 %all-gather.4.cloned.1.call-start = ((), (), s32[]{:S(2)}) async-start(), calls=%async_computation.5 | async-start | bytes 5308416 | tf_op jit(solution)/shard_map/all_gather | solution.py:95
  12.3 158.9 %reduce-scatter.4.cloned.1.call-start = ((), (), s32[]{:S(2)}) async-start(), calls=%async_computation.6 | async-start | bytes 5308416 | tf_op jit(solution)/shard_map/reduce_scatter | solution.py:108
  88.2 1.3 copy-start.4
  89.7 5.0 copy-start.6
  97.1 2.0 copy-start.12
  103.6 2.0 copy-start.12
  107.5 1.1 copy-start.8
  112.2 58.9 %copy-start.1 = (bf16[2,1,128,1152]{3,2,1,0:T(8,128)(2,1)S(1)}, bf16[2,1,128,1152]{3,2,1,0:T(8,128)(2,1)}, u32[]{:S(2)}) copy-start(bf16[2,1,128,1152]{3,2,1,0:T(8,128)(2,1)} %param.12) | copy-start | bytes 1769476
  112.3 148.8 %all-gather.6.cloned.1.call-start = ((), (), s32[]{:S(2)}) async-start(), calls=%async_computation.7 | async-start | bytes 5308416 | tf_op jit(solution)/shard_map/all_gather | solution.py:115
  171.2 2.9 copy-start.2
  174.5 28.9 %copy-start.11 = (f32[2,72]{1,0:T(2,128)S(1)}, f32[2,72]{1,0:T(2,128)}, u32[]{:S(2)}) copy-start(f32[2,72]{1,0:T(2,128)} %param.18) | copy-start | bytes 1732
  174.5 28.9 %copy-start.7 = (bf16[3,1152,144]{1,2,0:T(8,128)(2,1)S(1)}, bf16[3,1152,144]{1,2,0:T(8,128)(2,1)}, u32[]{:S(2)}) copy-start(bf16[3,1152,144]{1,2,0:T(8,128)(2,1)} %param.17) | copy-start | bytes 2985988
  203.1 157.8 %reduce-scatter.6.cloned.1.call-start = ((), (), s32[]{:S(2)}) async-start(), calls=%async_computation.8 | async-start | bytes 5308416 | tf_op jit(solution)/shard_map/reduce_scatter | solution.py:121
  289.3 2.4 copy-start.5
  292.4 2.6 copy-start.9
  302.0 148.3 %all-gather.8.cloned.1.call-start = ((), (), s32[]{:S(2)}) async-start(), calls=%async_computation.9 | async-start | bytes 5308416 | tf_op jit(solution)/shard_map/all_gather | solution.py:129
  389.5 1.1 copy-start.3
  392.4 128.2 %reduce-scatter.8.cloned.1.call-start = ((), (), s32[]{:S(2)}) async-start(), calls=%async_computation.10 | async-start | bytes 5308416 | tf_op jit(solution)/shard_map/reduce_scatter | solution.py:135
Sparse Core Ops, SparseCore 0:
  12.4 62.3 all-gather.3
  112.4 58.7 reduce-scatter.3
  203.2 57.7 all-gather.5
  302.1 58.7 reduce-scatter.5
  392.5 57.7 all-gather.7
  461.8 58.7 reduce-scatter.7
where the time goes:
time: 530 us; the launch traced here: 529 us
  waiting for transfers between devices  354 us (67%)
  matrix products  55.9 us (11%)
  blocking collectives  54.2 us (10%)
  local copies, waits for them, and re-layouts  28.9 us (5%)
  other arithmetic  18.6 us (4%)
  between operations  13.8 us (3%)
    reduce_scatter x3, waiting for transfers between devices, body(): lax.psum_scatter(partial_value.astype(jnp.bfloat16), 'tp', scatter_dimens...  177 us
    all_gather x2, waiting for transfers between devices, body(): lax.all_gather(normed, 'tp', axis=2, tiled=True)  120 us
    all_gather x1, waiting for transfers between devices, body(): lax.all_gather(moved_rows, 'tp', axis=2, tiled=True)  56.9 us
    all_to_all x1, blocking collectives, body(): lax.all_to_all(normed, 'seq', split_axis=2, concat_axis=1, tiled=True)  27.1 us
    all_to_all x1, blocking collectives, body(): lax.all_to_all(shares, 'seq', split_axis=1, concat_axis=2, tiled=True)  27.1 us
    dot_general x6, matrix products, project_heads(): jnp.einsum('bfpd,de->bfpe', rows_piece, table[which_part], preferred_elem...  26.8 us
    dot_general x1, matrix products, body(): jnp.einsum('bfpe,ed->bfpd', hidden, fc_out, preferred_element_type=jnp.fl...  11.3 us
  transfers between devices with their start and end apart: 6, of which 6 were waited for; matrix products, arithmetic and copies ran while one was open for 0% of the time, Pallas kernels for 0%

commit v1 on v0

--- a/solution.py
+++ b/solution.py
@@ -7,6 +7,13 @@
 D = 1152
 H = 16
 epsilon = 1e-06
+
+
+def raise_slot(packet, which_axis):
+    top = jnp.concatenate(
+        lax.all_to_all(jnp.stack(lax.psum(1, which_axis) * [packet]), which_axis, 0, 0), axis=2
+    )
+    return top
 
 
 def layer_norm(values):
@@ -125,10 +132,7 @@
     running = running + modulation[:, 5][:, None, None, :] * temporal_out.astype(jnp.float32)
     normed = modulated(running, modulation, 6)
     projected = jnp.einsum(
-        "bfpd,de->bfpe",
-        lax.all_gather(normed, "tp", axis=2, tiled=True),
-        fc_in,
-        preferred_element_type=jnp.float32,
+        "bfpd,de->bfpe", raise_slot(normed, "tp"), fc_in, preferred_element_type=jnp.float32
     )
     hidden = jax.nn.gelu(projected, approximate=True).astype(jnp.bfloat16)
     partial_value = jnp.einsum("bfpe,ed->bfpd", hidden, fc_out, preferred_element_type=jnp.float32)

time: 530 us -> 582 us (1.098)
  blocking collectives: 54.2 us -> 164 us
  waiting for transfers between devices: 354 us -> 293 us
    all_to_all x0 -> x1, blocking collectives: none -> 110 us  [raise_slot(): lax.all_to_all(jnp.stack(lax.psum(1, which_axis) * [packet]), which_axis,...]
    all_gather x2 -> x1, waiting for transfers between devices: 120 us -> 62.3 us  [body(): lax.all_gather(normed, 'tp', axis=2, tiled=True)]
  transfers between devices with their start and end apart: 6 -> 5, of which waited for: 6 -> 5; matrix products, arithmetic and copies ran while one was open for 0% -> 0% of each run, Pallas kernels for 0% -> 0%
where the time goes in v1:
time: 582 us; the launch traced here: 581 us
  waiting for transfers between devices  293 us (50%)
  blocking collectives  164 us (28%)
  matrix products  55.9 us (10%)
  local copies, waits for them, and re-layouts  32.2 us (6%)
  other arithmetic  17.8 us (3%)
  between operations  13.5 us (2%)
    reduce_scatter x3, waiting for transfers between devices, body(): lax.psum_scatter(partial_value.astype(jnp.bfloat16), 'tp', scatter_dimens...  174 us
    all_to_all x1, blocking collectives, raise_slot(): lax.all_to_all(jnp.stack(lax.psum(1, which_axis) * [packet]), which_axis,...  110 us
    all_gather x1, waiting for transfers between devices, body(): lax.all_gather(normed, 'tp', axis=2, tiled=True)  62.3 us
    all_gather x1, waiting for transfers between devices, body(): lax.all_gather(moved_rows, 'tp', axis=2, tiled=True)  56.9 us
    all_to_all x1, blocking collectives, body(): lax.all_to_all(normed, 'seq', split_axis=2, concat_axis=1, tiled=True)  27.1 us
    all_to_all x1, blocking collectives, body(): lax.all_to_all(shares, 'seq', split_axis=1, concat_axis=2, tiled=True)  27.1 us
    dot_general x6, matrix products, project_heads(): jnp.einsum('bfpd,de->bfpe', rows_piece, table[which_part], preferred_elem...  26.8 us
  transfers between devices with their start and end apart: 5, of which 5 were waited for; matrix products, arithmetic and copies ran while one was open for 0% of the time, Pallas kernels for 0%

profile of v1, /device:TPU:4, one launch (start us, length us, event | category | flops | bytes accessed | tf_op | source)
XLA Modules:
  0.0 580.9 jit_solution(8911568428961203966)
XLA Ops:
  6.5 0.9 slice_bitcast_fusion.1
  7.5 1.2 convert_reduce_fusion
  8.7 1.4 fusion.54
  10.1 2.2 fusion.57
  12.6 62.3 %all-gather.3.cloned.1.call-done = bf16[2,1,1024,1152]{3,2,0,1:T(8,128)(2,1)} async-done(((bf16[2,1,128,1152]{3,2,0,1:T(8,128)(2,1)}), bf16[2,1,1024,1152]{3,2,0,1:T(8,128)(2,1)}) %all-gather.3.cloned.1.call-update) | async-done | bytes 4718608 | tf_op jit(solution)/shard_map/all_gather | solution.py:102
  74.8 5.1 fusion.90
  79.9 1.4 reduce_sum.111
  81.3 5.5 fusion.91
  86.8 1.4 reduce_sum.112
  88.4 1.0 copy-done.4
  89.7 4.9 fusion.51
  94.6 12.8 %while.2 = (s32[]{:T(128)}, bf16[2,2,512,2,72]{2,4,3,1,0:T(8,128)(2,1)S(1)}, s32[2]{0:T(128)S(1)}, bf16[2,1024,2,72]{1,3,2,0:T(8,128)(2,1)S(1)}, bf16[2,1024,2,7...) while((s32[]{:T(128)}, ...), condition=%wide.region_6.7_spmd, body=%wide.region_4.6_spmd.sunk | while | flops 614610944 | bytes 20922552 | solution.py:72
  97.2 1.9 fusion.106
  99.1 1.9 fusion.107
  103.6 1.9 fusion.106
  105.5 1.9 fusion.107
  108.5 3.7 fusion.25
  112.3 58.9 %reduce-scatter.4.cloned.1.call-done = bf16[2,1,128,1152]{3,2,0,1:T(8,128)(2,1)} async-done(((bf16[2,1,1024,1152]{3,2,0,1:T(8,128)(2,1)}), bf16[2,1,128,1152]{3,2,0,1:T(8,128)(2,1)}) %reduce-scatter.4.cloned.1.call-update) | async-done | bytes 589840 | tf_op jit(solution)/shard_map/reduce_scatter | solution.py:115
  171.2 1.4 fusion.69
  172.6 1.4 multiply_reduce_fusion.3
  175.1 27.1 %all_to_all.26 = bf16[2,1,128,1152]{3,0,1,2:T(2,128)(2,1)S(1)} all-to-all(bf16[2,1,128,1152]{3,0,1,2:T(2,128)(2,1)S(1)} %copy.75), channel_id=1, replica_groups=mesh['seq'=32,'tp'=8] {'seq'}, dimensions={2} | all-to-all | bytes 1179648 | tf_op jit(solution)/shard_map/all_to_all | solution.py:120
  204.2 56.9 %all-gather.5.cloned.1.call-done = bf16[2,32,32,1152]{3,1,0,2:T(8,128)(2,1)} async-done(((bf16[2,32,4,1152]{3,1,0,2:T(8,128)(2,1)}), bf16[2,32,32,1152]{3,1,0,2:T(8,128)(2,1)}) %all-gather.5.cloned.1.call-update) | async-done | bytes 4718608 | tf_op jit(solution)/shard_map/all_gather | solution.py:122
  261.0 3.9 fusion.45
  265.0 1.4 reshape_reshape.10
  266.4 3.7 multiply_reduce_fusion
  270.1 3.7 multiply_reduce_fusion.1
  273.8 2.4 multiply_convert_fusion
  276.3 1.2 copy.82
  277.4 1.5 convert_element_type.121
  278.9 1.8 copy.83
  280.7 1.4 reshape_reshape.12
  282.1 2.4 copy.79
  284.5 1.5 convert_element_type.119
  286.0 1.8 copy.80
  287.8 1.4 reshape_reshape.11
  289.3 2.4 fusion.36
  292.4 1.1 copy.88
  293.5 1.5 reshape_reshape_transpose.3
  295.0 3.3 convolution_convert_fusion.1
  298.2 3.8 copy.90
  302.1 58.9 %reduce-scatter.6.cloned.1.call-done = bf16[2,32,4,1152]{3,1,0,2:T(8,128)(2,1)} async-done(((bf16[2,32,32,1152]{3,1,0,2:T(8,128)(2,1)}), bf16[2,32,4,1152]{3,1,0,2:T(8,128)(2,1)}) %reduce-scatter.6.cloned.1.call-update) | async-done | bytes 589840 | tf_op jit(solution)/shard_map/reduce_scatter | solution.py:128
  360.9 1.5 copy.91
  362.4 27.1 %all_to_all.27 = bf16[2,32,4,1152]{3,2,0,1:T(4,128)(2,1)S(1)} all-to-all(bf16[2,32,4,1152]{3,2,0,1:T(4,128)(2,1)S(1)} %copy.91), channel_id=1, replica_groups=mesh['seq'=32,'tp'=8] {'seq'}, dimensions={1} | all-to-all | bytes 1179648 | tf_op jit(solution)/shard_map/all_to_all | solution.py:131
  392.2 110.3 %all_to_all.28 = bf16[8,2,1,128,1152]{4,3,1,2,0:T(8,128)(2,1)S(1)} all-to-all(bf16[8,2,1,128,1152]{4,3,1,2,0:T(8,128)(2,1)S(1)} %stack.2), channel_id=1, replica_groups=mesh['seq'=32,'tp'=8] {'tp'}, dimensions={0} | all-to-all | bytes 9437184 | tf_op jit(solution)/shard_map/all_to_all | solution.py:14
  502.5 2.6 copy.95
  505.1 11.3 %fusion.26 = bf16[2,1,1024,1152]{3,2,0,1:T(8,128)(2,1)} fusion(bf16[2,1024,1152]{2,1,0:T(8,128)(2,1)} %bitcast.184, bf16[576,1152]{1,0:T(8,128)(2,1)S(1)} %copy-done, bf16[1152,576]{0,1:T(8,128)(2,1)} %param.20), kind=kOutput, calls=%fused_computation.32 | convolution fusion | flops 5448794112 | bytes 12091392 | tf_op jit(solution)/shard_map/bfpe,ed->bfpd/dot_general | solution.py:138
  516.4 55.9 %reduce-scatter.8.cloned.1.call-done = bf16[2,1,128,1152]{3,2,0,1:T(8,128)(2,1)} async-done(((bf16[2,1,1024,1152]{3,2,0,1:T(8,128)(2,1)}), bf16[2,1,128,1152]{3,2,0,1:T(8,128)(2,1)}) %reduce-scatter.8.cloned.1.call-update) | async-done | bytes 589840 | tf_op jit(solution)/shard_map/reduce_scatter | solution.py:139
  572.4 2.0 fusion.71
  (72 shorter events, 9.5 us)
Async XLA Ops:
  6.5 498.6 %copy-start = (bf16[576,1152]{1,0:T(8,128)(2,1)S(1)}, bf16[576,1152]{1,0:T(8,128)(2,1)}, u32[]{:S(2)}) copy-start(bf16[576,1152]{1,0:T(8,128)(2,1)} %param.21) | copy-start | bytes 3981316
  6.5 5.8 %copy-start.10 = (f32[2,72]{1,0:T(2,128)S(1)}, f32[2,72]{1,0:T(2,128)}, u32[]{:S(2)}) copy-start(f32[2,72]{1,0:T(2,128)} %param.15) | copy-start | bytes 1732
  6.5 68.3 %all-gather.3.cloned.1.call-start = ((), (), s32[]{:S(2)}) async-start(), calls=%async_computation.6 | async-start | bytes 5308416 | tf_op jit(solution)/shard_map/all_gather | solution.py:102
  12.3 158.9 %reduce-scatter.4.cloned.1.call-start = ((), (), s32[]{:S(2)}) async-start(), calls=%async_computation.7 | async-start | bytes 5308416 | tf_op jit(solution)/shard_map/reduce_scatter | solution.py:115
  88.2 1.3 copy-start.4
  89.7 5.0 copy-start.6
  97.1 2.0 copy-start.12
  103.6 2.0 copy-start.12
  107.5 1.1 copy-start.8
  112.2 58.9 %copy-start.1 = (bf16[2,1,128,1152]{3,2,1,0:T(8,128)(2,1)S(1)}, bf16[2,1,128,1152]{3,2,1,0:T(8,128)(2,1)}, u32[]{:S(2)}) copy-start(bf16[2,1,128,1152]{3,2,1,0:T(8,128)(2,1)} %param.12) | copy-start | bytes 1769476
  112.3 148.8 %all-gather.5.cloned.1.call-start = ((), (), s32[]{:S(2)}) async-start(), calls=%async_computation.8 | async-start | bytes 5308416 | tf_op jit(solution)/shard_map/all_gather | solution.py:122
  171.2 2.9 copy-start.2
  174.5 28.9 %copy-start.11 = (f32[2,72]{1,0:T(2,128)S(1)}, f32[2,72]{1,0:T(2,128)}, u32[]{:S(2)}) copy-start(f32[2,72]{1,0:T(2,128)} %param.18) | copy-start | bytes 1732
  174.5 28.9 %copy-start.7 = (bf16[3,1152,144]{1,2,0:T(8,128)(2,1)S(1)}, bf16[3,1152,144]{1,2,0:T(8,128)(2,1)}, u32[]{:S(2)}) copy-start(bf16[3,1152,144]{1,2,0:T(8,128)(2,1)} %param.17) | copy-start | bytes 2985988
  203.1 157.8 %reduce-scatter.6.cloned.1.call-start = ((), (), s32[]{:S(2)}) async-start(), calls=%async_computation.9 | async-start | bytes 5308416 | tf_op jit(solution)/shard_map/reduce_scatter | solution.py:128
  289.3 2.4 copy-start.5
  292.4 2.6 copy-start.9
  302.0 270.4 %reduce-scatter.8.cloned.1.call-start = ((), (), s32[]{:S(2)}) async-start(), calls=%async_computation.10 | async-start | bytes 5308416 | tf_op jit(solution)/shard_map/reduce_scatter | solution.py:139
  389.5 1.1 copy-start.3
Sparse Core Ops, SparseCore 0:
  12.4 62.3 all-gather.2
  112.4 58.7 reduce-scatter.3
  203.2 57.7 all-gather.4
  302.1 58.7 reduce-scatter.5
  516.5 55.7 reduce-scatter.7
